TPU v7x, 32 devices: a whole 2x2x4 slice. The times are simulated.
32 devices in a mesh: chan: 2 (over x), vis: 2 (over core), pix: 8 (over z, y).
Axes of the slice: x: 2, y: 2, z: 4, core: 2. Of those that a mesh axis runs over, the one named last changes fastest.
Arguments:
- response: bfloat16 [16384, 49152], P(('chan', 'vis'), 'pix'), parts along dimension 0, may hold values from -5 to 5
- vis_data: float32 [16384], P(('chan', 'vis')), parts along dimension 0, may hold values from -6 to 6
- baseline_of_row: int32 [8192], P('vis'), may hold values from 0 to 8191
- noise_class: int32 [8192], P('vis'), may hold values from 0 to 15
- baseline_weight: float32 [8192], replicated, may hold values from 0.25 to 4
- class_inv_var: float32 [32], P('chan'), parts along dimension 0, may hold values from 0.25 to 4
Outputs:
- sky_map: float32 [98304], P(('chan', 'pix')), parts along dimension 0
- psf: float32 [98304, 64], P(('chan', 'pix'), 'vis'), parts along dimension 0
There are 2 independent parts, one for each index of `chan`. A program takes and returns all parts, laid end to end along the dimension named above; an argument that names none is the same for every part. Nothing has to cross between parts.
Inputs may be any that keep to these rules, and one draw needn't show every extreme that they name: `baseline_of_row`: baseline index of each row.
All inputs are finite; a program needn't handle non-finite values.
Results may differ from a plain program's by a relative error of at most 0.0041.
Values may be sent and summed in bfloat16 or wider, within the bound.
A program may use at most 128 MiB of HBM per device.

v0:
```python
import jax
import jax.numpy as jnp
from jax import lax
from jax.sharding import PartitionSpec as P

PANEL_DEV = 8


def shards(response, vis_data, baseline_of_row, noise_class, baseline_weight, class_inv_var):
    classes = lax.broadcasted_iota(jnp.int32, (1, class_inv_var.shape[0]), 1)
    class_weight = jnp.sum(
        jnp.where(noise_class[:, None] == classes, class_inv_var[None, :], jnp.float32(0.0)), axis=1
    )
    weight_row = jnp.take(baseline_weight, baseline_of_row) * class_weight
    own_panel = response[:, :PANEL_DEV]
    pix_rows = response.shape[1]
    piece_cols = lax.all_gather(own_panel, "pix", axis=1, tiled=True)
    operand = (weight_row[:, None] * piece_cols.astype(jnp.float32)).astype(jnp.bfloat16)
    plain_f = piece_cols.astype(jnp.float32)
    beam_part = jnp.concatenate(
        [
            lax.dot_general(
                response, operand, (((0,), (0,)), ((), ())), preferred_element_type=jnp.float32
            ),
            jnp.sum(weight_row[:, None] * plain_f * plain_f, axis=0)[None, :],
        ],
        axis=0,
    )
    weighted_vis = (weight_row * vis_data).astype(jnp.bfloat16)
    dirty_part = jnp.dot(weighted_vis, response, preferred_element_type=jnp.float32)
    norm_part = jnp.sum(weight_row[:, None] * jnp.square(response.astype(jnp.float32)), axis=0)
    col_share = beam_part.shape[1] // lax.axis_size("vis")
    beam_all, dirty_map, pixel_norm = lax.psum((beam_part, dirty_part, norm_part), "vis")
    beam_rows = lax.dynamic_slice_in_dim(beam_all, lax.axis_index("vis") * col_share, col_share, 1)
    panel_scale = beam_rows[pix_rows]
    beam_rows = beam_rows[:pix_rows]
    sky_map = dirty_map / jnp.sqrt(pixel_norm)
    psf = beam_rows / jnp.sqrt(pixel_norm[:, None] * panel_scale[None, :])
    return (sky_map, psf)


def solution(mesh):
    placed = (P(("chan", "vis"), "pix"), P(("chan", "vis")), P("vis"), P("vis"), P(), P("chan"))
    return jax.shard_map(
        shards,
        mesh=mesh,
        in_specs=placed,
        out_specs=(P(("chan", "pix")), P(("chan", "pix"), "vis")),
        check_vma=False,
    )
```

profile of v0, /device:TPU:0, one launch (start us, length us, event | category | flops | bytes accessed | tf_op | source)
XLA Modules:
  0.0 140.9 jit_solution(5494770655249392284)
XLA Ops:
  7.2 0.0 copy-start
  7.2 0.0 all-reduce.3.cloned.1.call-start
  7.2 0.7 fusion.2
  8.0 1.3 slice.9
  9.2 0.3 copy.14
  9.6 33.0 %all_gather.3 = bf16[4096,64]{0,1:T(8,128)(2,1)S(1)} all-gather(bf16[4096,8]{0,1:T(8,128)(2,1)S(1)} %copy.14), channel_id=1, replica_groups=mesh['chan'=2,'vis'=2,'pix'=8] {'pix'}, dimensions={1}, use_global_device_ids=true | all-gather | bytes 589824 | tf_op jit(solution)/shard_map/all_gather | solution.py:17
  42.6 0.0 copy-done
  42.6 23.0 %gather_fusion = f32[4096]{0:T(1024)S(1)} fusion(f32[8192]{0:T(1024)S(1)} %copy-done, s32[4096]{0:T(1024)S(1)} %fusion.2), kind=kCustom, calls=%fused_computation | custom fusion | bytes 49152 | tf_op jit(solution)/shard_map/jit(_take)/gather | solution.py:14
  65.6 0.9 select_reduce_fusion
  66.5 0.8 multiply_convert_fusion.2
  67.2 19.8 %convolution_bitcast_fusion = f32[6144,64]{0,1:T(8,128)S(1)} fusion(bf16[4096,6144]{1,0:T(8,128)(2,1)} %param.6, bf16[4096,64]{0,1:T(8,128)(2,1)S(1)} %all_gather.3, f32[4096]{0:T(1024)S(1)} %get-tuple-element.5), kind=kOutput, calls=%fused_computation.2 | convolution fusion | flops 3222011904 | bytes 52445184 | tf_op jit(solution)/shard_map/dot_general | solution.py:22
  87.1 0.2 fusion
  87.3 0.1 copy.13
  87.4 1.3 pad_maximum_fusion
  88.7 0.0 all-reduce.3.cloned.1.call-update
  88.7 19.3 %multiply_reduce_fusion = f32[6144]{0:T(1024)S(1)} fusion(bf16[4096,6144]{1,0:T(8,128)(2,1)} %param.6, f32[4096]{0:T(1024)S(1)} %get-tuple-element.5), kind=kLoop, calls=%fused_computation.1 | loop fusion | flops 100657152 | bytes 50372608 | tf_op jit(solution)/shard_map/reduce_sum | solution.py:31
  108.0 18.9 %fusion.3 = f32[1,6144]{1,0:T(1,128)S(1)} fusion(bf16[4096,1]{0,1:T(2,128)(2,1)S(1)} %reshape.26, bf16[4096,6144]{1,0:T(8,128)(2,1)} %param.6), kind=kOutput, calls=%fused_computation.17 | convolution fusion | flops 50331648 | bytes 50364416 | tf_op jit(solution)/shard_map/dot_general | solution.py:30
  126.9 3.5 %all-reduce = (f32[6144]{0:T(1024)S(1)}, f32[6144]{0:T(1024)S(1)}) all-reduce(f32[6144]{0:T(1024)S(1)} %bitcast.7, f32[6144]{0:T(1024)S(1)} %multiply_reduce_fusion), channel_id=1, replica_groups=mesh['chan'=2,'vis'=2,'pix'=8] {'vis'}, use_global_device_ids=true, to_apply=%region_1.2 | all-reduce | flops 12288 | bytes 98304 | tf_op jit(solution)/shard_map/psum | solution.py:33
  130.4 0.6 rsqrt_multiply_fusion
  131.1 0.0 all-reduce.3.cloned.1.call-done
  131.1 0.8 dynamic-slice_reduce_fusion
  131.9 2.2 %dynamic-slice_multiply_fusion = f32[6144,32]{0,1:T(8,128)} fusion(f32[6145,64]{0,1:T(8,128)} %all-reduce.3.cloned.1.call-done, s32[]{:T(128)S(6)} %select_n.21, f32[32]{0:T(128)S(1)} %dynamic-slice_reduce_fusion, f32[6144]{0:T(1024)S(1)} %get-tuple-element.3), kind=kLoop, calls=%fused_computation.7 | loop fusion | flops 393216 | bytes 1597572 | tf_op jit(solution)/shard_map/div | solution.py:38
  (1 shorter events, 0.0 us)
Async XLA Ops:
  7.2 35.4 %copy-start = (f32[8192]{0:T(1024)S(1)}, f32[8192]{0:T(1024)}, u32[]{:S(2)}) copy-start(f32[8192]{0:T(1024)} %param.10) | copy-start | bytes 98308
  7.2 123.9 %all-reduce.3.cloned.1.call-start = ((), (), s32[]{:S(2)}) async-start(), calls=%async_computation | async-start | bytes 3211264 | tf_op jit(solution)/shard_map/psum | solution.py:33
Sparse Core Ops, SparseCore 0:
  88.8 21.5 all-reduce.2
where the time goes:
time: 142 us; the launch traced here: 141 us
  matrix products  38.7 us (27%)
  blocking collectives  36.6 us (26%)
  other arithmetic  26 us (18%)
  local copies, waits for them, and re-layouts  25.6 us (18%)
  between operations  14.1 us (10%)
    all_gather x1, blocking collectives, shards(): piece_cols = lax.all_gather(own_panel, 'pix', axis=1, tiled=True)  33 us
    gather x1, local copies, waits for them, and re-layouts, shards(): weight_row = jnp.take(baseline_weight, baseline_of_row) * class_weight  23 us
    dot_general x1, matrix products, shards(): lax.dot_general(response, operand, (((0,), (0,)), ((), ())), preferred_el...  19.8 us
    reduce_sum x1, other arithmetic, shards(): jnp.sum(weight_row[:, None] * jnp.square(response.astype(jnp.float32)), a...  19.3 us
    dot_general x1, matrix products, shards(): jnp.dot(weighted_vis, response, preferred_element_type=jnp.float32)  18.9 us
    psum x1, blocking collectives, shards(): lax.psum((beam_part, dirty_part, norm_part), 'vis')  3.53 us
  transfers between devices with their start and end apart: 1, of which 0 were waited for; matrix products, arithmetic and copies ran while one was open for 28% of the time, Pallas kernels for 0%

commit v1 on v0

v1 whole, which is shorter than its diff:
```python
import functools

import jax
import jax.numpy as jnp
from jax import lax
from jax.experimental import pallas as pl
from jax.experimental.pallas import tpu as pltpu
from jax.sharding import PartitionSpec as P

PANEL_DEV = 8
LANES = 128
EXTRA = 16
MESH_ID = pl.DeviceIdType.MESH
F32, BF16 = jnp.float32, jnp.bfloat16


def kernel(
    n_pix, n_early,
    resp, vis_h, base_h, cls_h, bw_h, civ_h,
    sky_h, psf_h,
    x, vis, base, cls, bw, civ, pbuf, w_ref, w2, lhs, nbuf, keep, sbuf, rbuf,
    qpart, qown, qrecv, psf, sky,
    in_sem, small_sem, psend, precv, vsend, vrecv, qsem, out_sem,
):
    n_chunk, rows, ch = x.shape
    n_panel = n_pix * PANEL_DEV
    half = n_panel // 2
    me = lax.axis_index("pix")
    v = lax.axis_index("vis")
    other = 1 - v

    first = pltpu.make_async_copy(
        resp.at[:, pl.ds(0, LANES)], x.at[0, :, pl.ds(0, LANES)], in_sem.at[n_chunk]
    )
    first.start()
    smalls = [
        pltpu.make_async_copy(a, b, small_sem.at[i])
        for i, (a, b) in enumerate(
            [(vis_h, vis), (base_h, base), (cls_h, cls), (bw_h, bw), (civ_h, civ)]
        )
    ]
    for c in smalls:
        c.start()
    rest = None
    if ch > LANES:
        rest = pltpu.make_async_copy(
            resp.at[:, pl.ds(LANES, ch - LANES)],
            x.at[0, :, pl.ds(LANES, ch - LANES)],
            in_sem.at[0],
        )
        rest.start()

    def chunk_copy(c):
        return pltpu.make_async_copy(
            resp.at[:, pl.ds(pl.multiple_of(c * ch, ch), ch)], x.at[c], in_sem.at[c]
        )

    for c in range(1, n_chunk):
        chunk_copy(c).start()

    barrier = pltpu.get_barrier_semaphore()

    def greet(d, carry):
        pl.semaphore_signal(
            barrier, inc=1, device_id={"pix": lax.rem(me + d, n_pix)}, device_id_type=MESH_ID
        )
        return carry

    lax.fori_loop(1, n_pix, greet, 0)
    pl.semaphore_signal(barrier, inc=1, device_id={"vis": other}, device_id_type=MESH_ID)

    first.wait()
    pick = (
        lax.broadcasted_iota(jnp.int32, (16, LANES), 0)
        == lax.broadcasted_iota(jnp.int32, (16, LANES), 1)
    ).astype(BF16)
    own = lax.dot_general(
        pick, x[0, :, :LANES], (((1,), (1,)), ((), ())), preferred_element_type=F32
    )
    pbuf[me] = own[:PANEL_DEV].astype(BF16)
    pl.semaphore_wait(barrier, n_pix)

    def panel_copy(slot, peer):
        return pltpu.make_async_remote_copy(
            src_ref=pbuf.at[slot], dst_ref=pbuf.at[slot],
            send_sem=psend.at[peer], recv_sem=precv.at[slot],
            device_id={"pix": peer}, device_id_type=MESH_ID,
        )

    def send_panel(d, carry):
        panel_copy(me, lax.rem(me + d, n_pix)).start()
        return carry

    lax.fori_loop(1, n_pix, send_panel, 0)

    for c in smalls:
        c.wait()
    n_hi = bw.shape[0]
    t0 = bw[...].astype(BF16)
    left = bw[...] - t0.astype(F32)
    t1 = left.astype(BF16)
    t2 = (left - t1.astype(F32)).astype(BF16)
    table = jnp.concatenate([t0, t1, t2], axis=0)
    n_cls = civ.shape[1]
    diag = lax.broadcasted_iota(jnp.int32, (n_cls, n_cls), 0) == lax.broadcasted_iota(
        jnp.int32, (n_cls, n_cls), 1
    )
    civ_col = jnp.sum(
        jnp.where(diag, jnp.broadcast_to(civ[...], (n_cls, n_cls)), 0.0), axis=1, keepdims=True
    )
    step = min(rows, 512)

    def weights(i, carry):
        cols = pl.ds(pl.multiple_of(i * step, step), step)
        idx = base[:, cols]
        hi = lax.broadcast_in_dim(idx // LANES, (n_hi, step), (0, 1))
        lo = lax.broadcast_in_dim(lax.rem(idx, LANES), (LANES, step), (0, 1))
        hot = (hi == lax.broadcasted_iota(jnp.int32, (n_hi, step), 0)).astype(F32).astype(BF16)
        picked = lax.dot_general(
            table, jnp.concatenate([hot] * 3, axis=0), (((0,), (0,)), ((), ())),
            preferred_element_type=F32,
        )
        bw_row = jnp.sum(
            jnp.where(lo == lax.broadcasted_iota(jnp.int32, (LANES, step), 0), picked, 0.0),
            axis=0, keepdims=True,
        )
        kinds = lax.broadcast_in_dim(cls[:, cols], (n_cls, step), (0, 1))
        cw_row = jnp.sum(
            jnp.where(
                kinds == lax.broadcasted_iota(jnp.int32, (n_cls, step), 0), civ_col, 0.0
            ),
            axis=0, keepdims=True,
        )
        w = bw_row * cw_row
        w_ref[:, cols] = w
        w_hi = w.astype(BF16).astype(F32)
        at = lax.broadcasted_iota(jnp.int32, (EXTRA, step), 0)
        w2[:, cols] = jnp.where(
            at == 0, w_hi, jnp.where(at == 1, w - w_hi, 0.0)
        ).astype(BF16)
        lhs[n_panel:, cols] = jnp.where(at == 0, w * vis[:, cols], 0.0).astype(BF16)
        return carry

    lax.fori_loop(0, rows // step, weights, 0)

    kb = min(rows, 512)

    def norm_of(c):
        acc = None
        for k in range(0, rows, kb):
            xb = x[c, k : k + kb, :]
            part = jnp.dot(w2[:, k : k + kb], xb * xb, preferred_element_type=F32)
            acc = part if acc is None else acc + part
        nbuf[c] = jnp.broadcast_to(jnp.sum(acc, axis=0, keepdims=True), (8, ch))

    def vis_copy(c):
        return pltpu.make_async_remote_copy(
            src_ref=sbuf.at[c], dst_ref=rbuf.at[c],
            send_sem=vsend.at[c], recv_sem=vrecv.at[c],
            device_id={"vis": other}, device_id_type=MESH_ID,
        )

    def beam_of(c):
        res = jnp.dot(lhs[...], x[c], preferred_element_type=F32)
        at = lax.broadcasted_iota(jnp.int32, (8, ch), 0)
        pair = jnp.where(
            at == 0, res[n_panel : n_panel + 8], jnp.where(at == 1, nbuf[c], 0.0)
        )
        keep[c, :half] = res[:half]
        keep[c, half:] = pair
        sbuf[c, :half] = res[half:n_panel]
        sbuf[c, half:] = pair
        vis_copy(c).start()

    if rest is not None:
        rest.wait()
    norm_of(0)

    def early(c, carry):
        chunk_copy(c).wait()
        norm_of(c)
        return carry

    lax.fori_loop(1, n_early, early, 0)

    def wait_panel(d, carry):
        slot = lax.rem(me + d, n_pix)
        panel_copy(slot, slot).wait_recv()
        return carry

    lax.fori_loop(1, n_pix, wait_panel, 0)

    def weigh(j, carry):
        w = w_ref[...]
        src = lax.rem(2 * j + v * (n_pix // 2), n_pix)
        a = pbuf[src].astype(F32)
        b = pbuf[src + 1].astype(F32)
        wa, wb = w * a, w * b
        lhs[pl.ds(pl.multiple_of(j * 16, 16), 16), :] = jnp.concatenate([wa, wb], axis=0).astype(
            BF16
        )
        sq = jnp.concatenate(
            [
                jnp.sum(wa * a, axis=1, keepdims=True),
                jnp.sum(wb * b, axis=1, keepdims=True),
            ],
            axis=0,
        )
        qpart[pl.ds(pl.multiple_of(j * 16, 16), 16), :] = jnp.broadcast_to(sq, (16, LANES))
        return carry

    lax.fori_loop(0, n_pix // 2, weigh, 0)
    q_copy = pltpu.make_async_remote_copy(
        src_ref=qpart.at[pl.ds(half, half)], dst_ref=qrecv,
        send_sem=qsem.at[0], recv_sem=qsem.at[1],
        device_id={"vis": other}, device_id_type=MESH_ID,
    )
    q_copy.start()

    def backlog(c, carry):
        beam_of(c)
        return carry

    lax.fori_loop(0, n_early, backlog, 0)

    def late(c, carry):
        chunk_copy(c).wait()
        norm_of(c)
        beam_of(c)
        return carry

    lax.fori_loop(n_early, n_chunk, late, 0)

    q_copy.wait()
    qown[...] = lax.rsqrt(qpart[:half, :1] + qrecv[:, :1]) * jnp.ones((1, LANES), F32)

    def out_copies(c):
        cols = pl.ds(pl.multiple_of(c * ch, ch), ch)
        return (
            pltpu.make_async_copy(psf.at[c], psf_h.at[:, cols], out_sem.at[0, c]),
            pltpu.make_async_copy(sky.at[c], sky_h.at[:, cols], out_sem.at[1, c]),
        )

    def final(c, carry):
        vis_copy(c).wait_recv()
        pair = keep[c, half:] + rbuf[c, half:]
        scale = lax.rsqrt(pair[1:2])
        sky[c] = pair[0:1] * scale
        psf[c] = (keep[c, :half] + rbuf[c, :half]) * scale * qown[:, :1]
        for o in out_copies(c):
            o.start()
        return carry

    lax.fori_loop(0, n_chunk, final, 0)

    def drain(c, carry):
        vis_copy(c).wait_send()
        for o in out_copies(c):
            o.wait()
        return carry

    lax.fori_loop(0, n_chunk, drain, 0)

    def drain_panel(d, carry):
        panel_copy(me, lax.rem(me + d, n_pix)).wait_send()
        return carry

    lax.fori_loop(1, n_pix, drain_panel, 0)


def shards(n_pix, response, vis_data, baseline_of_row, noise_class, baseline_weight, class_inv_var):
    rows, pix = response.shape
    ch = next(c for c in (512, 256, 128) if pix % c == 0)
    n_chunk = pix // ch
    n_early = max(1, n_chunk // 2)
    n_panel = n_pix * PANEL_DEV
    half = n_panel // 2
    n_hi = baseline_weight.shape[0] // LANES
    n_cls = class_inv_var.shape[0]
    vmem, dma = pltpu.VMEM, pltpu.SemaphoreType.DMA
    any_space = pl.BlockSpec(memory_space=pl.ANY)
    sky, psf = pl.pallas_call(
        functools.partial(kernel, n_pix, n_early),
        out_shape=(
            jax.ShapeDtypeStruct((1, pix), F32),
            jax.ShapeDtypeStruct((half, pix), F32),
        ),
        in_specs=[any_space] * 6,
        out_specs=(any_space, any_space),
        scratch_shapes=[
            vmem((n_chunk, rows, ch), BF16),
            vmem((1, rows), F32),
            vmem((1, rows), jnp.int32),
            vmem((1, rows), jnp.int32),
            vmem((n_hi, LANES), F32),
            vmem((1, n_cls), F32),
            vmem((n_pix, PANEL_DEV, rows), BF16),
            vmem((1, rows), F32),
            vmem((EXTRA, rows), BF16),
            vmem((n_panel + EXTRA, rows), BF16),
            vmem((n_chunk, 8, ch), F32),
            vmem((n_chunk, half + 8, ch), F32),
            vmem((n_chunk, half + 8, ch), F32),
            vmem((n_chunk, half + 8, ch), F32),
            vmem((n_panel, LANES), F32),
            vmem((half, LANES), F32),
            vmem((half, LANES), F32),
            vmem((n_chunk, half, ch), F32),
            vmem((n_chunk, 1, ch), F32),
            dma((n_chunk + 1,)),
            dma((5,)),
            dma((n_pix,)),
            dma((n_pix,)),
            dma((n_chunk,)),
            dma((n_chunk,)),
            dma((2,)),
            dma((2, n_chunk)),
        ],
        compiler_params=pltpu.CompilerParams(
            collective_id=0, has_side_effects=True, vmem_limit_bytes=63 * 1024 * 1024
        ),
    )(
        response,
        vis_data.reshape(1, rows),
        baseline_of_row.reshape(1, rows),
        noise_class.reshape(1, rows),
        baseline_weight.reshape(n_hi, LANES),
        class_inv_var.reshape(1, n_cls),
    )
    return sky.reshape(pix), psf.T


def solution(mesh):
    placed = (P(("chan", "vis"), "pix"), P(("chan", "vis")), P("vis"), P("vis"), P(), P("chan"))
    return jax.shard_map(
        functools.partial(shards, mesh.shape["pix"]),
        mesh=mesh,
        in_specs=placed,
        out_specs=(P(("chan", "pix")), P(("chan", "pix"), "vis")),
        check_vma=False,
    )
```

time: 142 us -> 41.5 us (0.29)
  matrix products: 38.7 us -> 0 us
  Pallas kernels: 0 us -> 37 us
  blocking collectives: 36.6 us -> 0 us
  other arithmetic: 26 us -> 0 us
  local copies, waits for them, and re-layouts: 25.6 us -> 3.41 us
  between operations: 14.1 us -> 0.64 us
    dot_general x2 -> x0, matrix products: 38.7 us -> none  [the longest x1 19.8 us: shards(): lax.dot_general(response, operand, (((0,), (0,)), ((), ())), preferred_el...]
    pallas_call x0 -> x1, Pallas kernels: none -> 37 us  [shards(): pl.pallas_call(functools.partial(kernel, n_pix, n_early), out_shape=(jax....]
    all_gather x1 -> x0, blocking collectives: 33 us -> none  [shards(): piece_cols = lax.all_gather(own_panel, 'pix', axis=1, tiled=True)]
    gather x1 -> x0, local copies, waits for them, and re-layouts: 23 us -> none  [shards(): weight_row = jnp.take(baseline_weight, baseline_of_row) * class_weight]
    reduce_sum x3 -> x0, other arithmetic: 20.4 us -> none  [the longest x1 19.3 us: shards(): jnp.sum(weight_row[:, None] * jnp.square(response.astype(jnp.float32)), a...]
    psum x1 -> x0, blocking collectives: 3.53 us -> none  [shards(): lax.psum((beam_part, dirty_part, norm_part), 'vis')]
    unnamed x3 -> x2, local copies, waits for them, and re-layouts: 0.32 us -> 3.41 us
    div x2 -> x0, other arithmetic: 2.81 us -> none  [the longest x1 2.19 us: shards(): psf = beam_rows / jnp.sqrt(pixel_norm[:, None] * panel_scale[None, :])]
  transfers between devices with their start and end apart: 1 -> 0, of which waited for: 0 -> 0; matrix products, arithmetic and copies ran while one was open for 28% -> 0% of each run, Pallas kernels for 0% -> 0%
where the time goes in v1:
time: 41.5 us; the launch traced here: 41.1 us
  Pallas kernels  37 us (89%)
  local copies, waits for them, and re-layouts  3.41 us (8%)
  between operations  0.64 us (2%)
    pallas_call x1, Pallas kernels, shards(): pl.pallas_call(functools.partial(kernel, n_pix, n_early), out_shape=(jax....  37 us
    unnamed x2, local copies, waits for them, and re-layouts  3.41 us

profile of v1, /device:TPU:0, one launch (start us, length us, event | category | flops | bytes accessed | tf_op | source)
XLA Modules:
  0.0 41.1 jit_solution(5700840062858367277)
XLA Ops:
  0.6 37.0 %shard_map.77 = (f32[1,6144]{1,0:T(1,128)}, f32[32,6144]{1,0:T(8,128)}) custom-call(bf16[4096,6144]{1,0:T(8,128)(2,1)} %resp.1, f32[1,4096]{1,0:T(1,128)} %bitcast.10, s32[1,4096]{1,0:T(1,128)} %bitcast.11, s32[1,4096]{1,0:T(1,128)} %bitcast.12, f32[64,128]{1,0:T(8,128)} %bitcast.8, f32[1,16]{1,0:T(1,128)} %bitcast.13), custom_call_target="tpu_custom_call" | custom-call | tf_op jit(solution)/shard_map/pallas_call | solution.py:282
  37.7 1.3 %copy.10 = f32[6144]{0:T(1024)} copy(f32[6144]{0:T(1024)} %bitcast.9) | data formatting | bytes 49152
  39.0 2.1 %copy.11 = f32[6144,32]{0,1:T(8,128)} copy(f32[6144,32]{0,1:T(8,128)} %bitcast.7) | data formatting | bytes 1572864

commit v2 on v1

--- a/solution.py
+++ b/solution.py
@@ -17,10 +17,10 @@
 def kernel(
     n_pix, n_early,
     resp, vis_h, base_h, cls_h, bw_h, civ_h,
-    sky_h, psf_h,
+    sky, psf,
     x, vis, base, cls, bw, civ, pbuf, w_ref, w2, lhs, nbuf, keep, sbuf, rbuf,
-    qpart, qown, qrecv, psf, sky,
-    in_sem, small_sem, psend, precv, vsend, vrecv, qsem, out_sem,
+    qpart, qown, qrecv,
+    in_sem, small_sem, psend, precv, vsend, vrecv, qsem,
 ):
     n_chunk, rows, ch = x.shape
     n_panel = n_pix * PANEL_DEV
@@ -223,40 +223,36 @@
 
     lax.fori_loop(0, n_early, backlog, 0)
 
+    q_copy.wait()
+    qown[...] = lax.rsqrt(qpart[:half, :1] + qrecv[:, :1]) * jnp.ones((1, LANES), F32)
+
+    def final(c, carry):
+        vis_copy(c).wait_recv()
+        cols = pl.ds(pl.multiple_of(c * ch, ch), ch)
+        pair = keep[c, half:] + rbuf[c, half:]
+        scale = lax.rsqrt(pair[1:2])
+        sky[:, cols] = pair[0:1] * scale
+        psf[:, cols] = (keep[c, :half] + rbuf[c, :half]) * scale * qown[:, :1]
+        return carry
+
+    lax.fori_loop(0, n_early, final, 0)
+
     def late(c, carry):
         chunk_copy(c).wait()
         norm_of(c)
         beam_of(c)
+
+        @pl.when(c > n_early)
+        def _():
+            final(c - 1, 0)
+
         return carry
 
     lax.fori_loop(n_early, n_chunk, late, 0)
-
-    q_copy.wait()
-    qown[...] = lax.rsqrt(qpart[:half, :1] + qrecv[:, :1]) * jnp.ones((1, LANES), F32)
-
-    def out_copies(c):
-        cols = pl.ds(pl.multiple_of(c * ch, ch), ch)
-        return (
-            pltpu.make_async_copy(psf.at[c], psf_h.at[:, cols], out_sem.at[0, c]),
-            pltpu.make_async_copy(sky.at[c], sky_h.at[:, cols], out_sem.at[1, c]),
-        )
-
-    def final(c, carry):
-        vis_copy(c).wait_recv()
-        pair = keep[c, half:] + rbuf[c, half:]
-        scale = lax.rsqrt(pair[1:2])
-        sky[c] = pair[0:1] * scale
-        psf[c] = (keep[c, :half] + rbuf[c, :half]) * scale * qown[:, :1]
-        for o in out_copies(c):
-            o.start()
-        return carry
-
-    lax.fori_loop(0, n_chunk, final, 0)
+    final(n_chunk - 1, 0)
 
     def drain(c, carry):
         vis_copy(c).wait_send()
-        for o in out_copies(c):
-            o.wait()
         return carry
 
     lax.fori_loop(0, n_chunk, drain, 0)
@@ -270,23 +266,22 @@
 
 def shards(n_pix, response, vis_data, baseline_of_row, noise_class, baseline_weight, class_inv_var):
     rows, pix = response.shape
-    ch = next(c for c in (512, 256, 128) if pix % c == 0)
+    ch = next(c for c in (1024, 768, 512, 256, 128) if pix % c == 0)
     n_chunk = pix // ch
-    n_early = max(1, n_chunk // 2)
+    n_early = max(1, n_chunk // 3)
     n_panel = n_pix * PANEL_DEV
     half = n_panel // 2
     n_hi = baseline_weight.shape[0] // LANES
     n_cls = class_inv_var.shape[0]
     vmem, dma = pltpu.VMEM, pltpu.SemaphoreType.DMA
-    any_space = pl.BlockSpec(memory_space=pl.ANY)
     sky, psf = pl.pallas_call(
         functools.partial(kernel, n_pix, n_early),
         out_shape=(
-            jax.ShapeDtypeStruct((1, pix), F32),
-            jax.ShapeDtypeStruct((half, pix), F32),
+            pltpu.VMEM((1, pix), F32),
+            pltpu.VMEM((half, pix), F32),
         ),
-        in_specs=[any_space] * 6,
-        out_specs=(any_space, any_space),
+        in_specs=[pl.BlockSpec(memory_space=pltpu.HBM)] * 6,
+        out_specs=(pl.BlockSpec(memory_space=pltpu.VMEM),) * 2,
         scratch_shapes=[
             vmem((n_chunk, rows, ch), BF16),
             vmem((1, rows), F32),
@@ -305,8 +300,6 @@
             vmem((n_panel, LANES), F32),
             vmem((half, LANES), F32),
             vmem((half, LANES), F32),
-            vmem((n_chunk, half, ch), F32),
-            vmem((n_chunk, 1, ch), F32),
             dma((n_chunk + 1,)),
             dma((5,)),
             dma((n_pix,)),
@@ -314,10 +307,9 @@
             dma((n_chunk,)),
             dma((n_chunk,)),
             dma((2,)),
-            dma((2, n_chunk)),
         ],
         compiler_params=pltpu.CompilerParams(
-            collective_id=0, has_side_effects=True, vmem_limit_bytes=63 * 1024 * 1024
+            collective_id=0, has_side_effects=True, vmem_limit_bytes=58 * 1024 * 1024
         ),
     )(
         response,

time: 41.5 us -> 37.4 us (0.901)
  Pallas kernels: 37 us -> 35 us
  local copies, waits for them, and re-layouts: 3.41 us -> 1.49 us
    pallas_call x1, Pallas kernels: 37 us -> 35 us  [shards(): pl.pallas_call(functools.partial(kernel, n_pix, n_early), out_shape=(pltp...]
    unnamed x2, local copies, waits for them, and re-layouts: 3.41 us -> 1.49 us
where the time goes in v2:
time: 37.4 us; the launch traced here: 37.1 us
  Pallas kernels  35 us (94%)
  local copies, waits for them, and re-layouts  1.49 us (4%)
  between operations  0.64 us (2%)
    pallas_call x1, Pallas kernels, shards(): pl.pallas_call(functools.partial(kernel, n_pix, n_early), out_shape=(pltp...  35 us
    unnamed x2, local copies, waits for them, and re-layouts  1.49 us

profile of v2, /device:TPU:0, one launch (start us, length us, event | category | flops | bytes accessed | tf_op | source)
XLA Modules:
  0.0 37.1 jit_solution(501479164981112291)
XLA Ops:
  0.6 35.0 %shard_map.77 = (f32[1,6144]{1,0:T(1,128)S(1)}, f32[32,6144]{1,0:T(8,128)S(1)}) custom-call(bf16[4096,6144]{1,0:T(8,128)(2,1)} %resp.1, f32[1,4096]{1,0:T(1,128)} %bitcast.10, s32[1,4096]{1,0:T(1,128)} %bitcast.11, s32[1,4096]{1,0:T(1,128)} %bitcast.12, f32[64,128]{1,0:T(8,128)} %bitcast.9, f32[1,16]{1,0:T(1,128)} %bitcast.13), custom_call_target="tpu_custom_call" | custom-call | tf_op jit(solution)/shard_map/pallas_call | solution.py:277
  35.6 0.6 %copy.10 = f32[6144]{0:T(1024)} copy(f32[6144]{0:T(1024)S(1)} %bitcast.8) | data formatting | bytes 49152
  36.2 0.9 %copy.11 = f32[6144,32]{0,1:T(8,128)} copy(f32[6144,32]{0,1:T(8,128)S(1)} %bitcast.7) | data formatting | bytes 1572864
